TPU v7x, 32 devices: a whole 2x2x4 slice. The times are simulated.
32 devices in a mesh: scen: 16 (over z, y, x), fac: 2 (over core).
Axes of the slice: x: 2, y: 2, z: 4, core: 2. Of those that a mesh axis runs over, the one named last changes fastest.
Arguments:
- scenarios: bfloat16 [256, 8192], P(('scen', 'fac')), may hold values from -40 to 40
Outputs:
- shrunk: float32 [8192, 8192], P('scen', 'fac')
- shrinkage: float32 [], replicated
- col_mean: float32 [8192], P('fac')
All inputs are finite; a program needn't handle non-finite values.
Results may differ from a plain program's by a relative error of at most 0.0008.
Values may be sent and summed in bfloat16 or wider, within the bound.
A program may use at most 64 MiB of HBM per device.

v0:
```python
import jax
import jax.numpy as jnp
from jax import lax
from jax.sharding import PartitionSpec as P


def on_device(scenarios):
    row_count = scenarios.shape[0]
    factors = scenarios.shape[1]
    scen_size = lax.axis_size("scen")
    fac_size = lax.axis_size("fac")
    total_rows = row_count * scen_size * fac_size
    group_width = factors // scen_size
    block_width = factors // fac_size
    owner_idx = lax.axis_index("scen")
    block_idx = lax.axis_index("fac")
    col_total = lax.psum(jnp.sum(scenarios.astype(jnp.float32), axis=0), ("scen", "fac"))
    col_mean = col_total / total_rows
    centered = (scenarios.astype(jnp.float32) - col_mean).astype(jnp.bfloat16)
    as_float = centered.astype(jnp.float32)
    squared = jnp.sum(as_float * as_float, axis=1)
    trace_part = jnp.sum(squared)
    fourth_part = jnp.sum(squared * squared)
    trace_total, fourth_total = lax.psum((trace_part, fourth_part), ("scen", "fac"))
    contract = (((0,), (0,)), ((), ()))
    local_rows = lax.all_gather(centered, "fac", axis=0, tiled=True)
    narrow_all = lax.all_to_all(local_rows, "scen", split_axis=1, concat_axis=0, tiled=True)
    wide_cols = lax.dynamic_slice_in_dim(local_rows, block_idx * block_width, block_width, 1)
    summed = lax.dot_general(
        narrow_all,
        lax.all_gather(wide_cols, "scen", axis=0, tiled=True),
        contract,
        preferred_element_type=jnp.float32,
    )
    covariance = summed / total_rows
    row_index = owner_idx * group_width + lax.broadcasted_iota(
        jnp.int32, (group_width, block_width), 0
    )
    col_index = block_idx * block_width + lax.broadcasted_iota(
        jnp.int32, (group_width, block_width), 1
    )
    diag_mask = (row_index == col_index).astype(jnp.float32)
    mu_scale = trace_total / (total_rows * factors)
    distance = covariance - mu_scale * diag_mask
    frob_sum = lax.psum(jnp.sum(distance * distance), ("scen", "fac"))
    spread = frob_sum / factors
    norm_sq = factors * (spread + mu_scale * mu_scale)
    beta_value = (fourth_total / total_rows - norm_sq) / (factors * total_rows)
    shrinkage = beta_value / spread
    shrunk = (1.0 - shrinkage) * covariance + shrinkage * mu_scale * diag_mask
    mean_block = lax.dynamic_slice_in_dim(col_mean, block_idx * block_width, block_width, 0)
    return (shrunk, shrinkage, mean_block)


def solution(mesh):
    return jax.shard_map(
        on_device,
        mesh=mesh,
        in_specs=(P(("scen", "fac"), None),),
        out_specs=(P("scen", "fac"), P(), P("fac")),
        check_vma=False,
    )
```

profile of v0, /device:TPU:0, one launch (start us, length us, event | category | flops | bytes accessed | tf_op | source)
XLA Modules:
  0.0 179.8 jit_solution(12894808986534440513)
XLA Ops:
  7.2 0.0 all-gather.2.cloned.1.call-start
  7.2 1.0 convert_reduce_fusion
  8.2 42.1 %psum.28 = f32[8192]{0:T(1024)S(1)} all-reduce(f32[8192]{0:T(1024)S(1)} %convert_reduce_fusion), channel_id=1, replica_groups=mesh['scen'=16,'fac'=2] {'scen','fac'}, use_global_device_ids=true, to_apply=%region_1.0 | all-reduce | flops 8192 | bytes 65536 | tf_op jit(solution)/shard_map/psum | solution.py:17
  50.4 1.6 fusion.5
  52.0 2.0 %all_gather.6 = bf16[16,8192]{1,0:T(8,128)(2,1)S(1)} all-gather(bf16[8,8192]{1,0:T(8,128)(2,1)S(1)} %get-tuple-element.7), channel_id=1, replica_groups=mesh['scen'=16,'fac'=2] {'fac'}, dimensions={0}, use_global_device_ids=true | all-gather | bytes 393216 | tf_op jit(solution)/shard_map/all_gather | solution.py:26
  54.0 0.7 constant_dynamic-slice_fusion
  54.6 0.0 all-gather.2.cloned.1.call-update
  54.6 0.7 copy.8
  55.4 5.4 %all-to-all-start = ((bf16[16,16,512]{2,0,1:T(8,128)(2,1)}), bf16[16,16,512]{2,0,1:T(8,128)(2,1)S(1)}, u32[]{:S(2)}, u32[]{:S(2)}) async-start(bf16[16,16,512]{2,0,1:T(8,128)(2,1)} %bitcast.8), calls=%async_computation | async-start | bytes 524288 | tf_op jit(solution)/shard_map/all_to_all | solution.py:27
  60.8 41.2 %psum.30 = f32[]{:T(128)} all-reduce(f32[]{:T(128)} %get-tuple-element.3), channel_id=1, replica_groups=mesh['scen'=16,'fac'=2] {'scen','fac'}, use_global_device_ids=true, to_apply=%region_6.0 | all-reduce | flops 1 | bytes 8 | tf_op jit(solution)/shard_map/psum | solution.py:24
  102.0 0.6 dynamic_slice.7
  104.6 0.7 multiply_reduce_fusion
  105.2 0.0 all-to-all-done
  105.2 10.7 %all-gather.2.cloned.1.call-done = bf16[256,4096]{1,0:T(8,128)(2,1)} async-done(((bf16[16,4096]{1,0:T(8,128)(2,1)}), bf16[256,4096]{1,0:T(8,128)(2,1)}) %all-gather.2.cloned.1.call-update) | async-done | bytes 2097168 | tf_op jit(solution)/shard_map/all_gather | solution.py:31
  115.9 6.8 %fusion.2 = (f32[]{:T(128)}, f32[512,4096]{1,0:T(8,128)}) fusion(f32[]{:T(128)S(6)} %div.32, s32[4096]{0:T(1024)S(1)} %iota_add_fusion, s32[512]{0:T(512)S(1)} %iota_add_fusion.1, bf16[256,512]{1,0:T(8,128)(2,1)S(1)} %bitcast.10, bf16[256,4096]{1,0:T(8,128)(2,1)} %all-gather.2.cloned.1.call-done), kind=kOutput, calls=%fused_computation.4 | convolution fusion | flops 1086324736 | bytes 10766344 | tf_op jit(solution)/shard_map/dot_general | solution.py:29
  122.8 39.0 %all-reduce = (f32[]{:T(128)}, f32[]{:T(128)}) all-reduce(f32[]{:T(128)} %multiply_reduce_fusion, f32[]{:T(128)} %get-tuple-element.8), channel_id=1, replica_groups=mesh['scen'=16,'fac'=2] {'scen','fac'}, use_global_device_ids=true, to_apply=%region_4.0 | all-reduce | flops 2 | bytes 16 | tf_op jit(solution)/shard_map/psum | solution.py:24
  163.1 8.7 %fusion.3 = f32[512,4096]{1,0:T(8,128)} fusion(f32[512,4096]{1,0:T(8,128)} %get-tuple-element.9, f32[]{:T(128)S(6)} %mul.61, f32[]{:T(128)S(6)} %mul.58, s32[4096]{0:T(1024)S(1)} %iota_add_fusion, s32[512]{0:T(512)S(1)} %iota_add_fusion.1), kind=kLoop, calls=%fused_computation.5 | loop fusion | flops 8388608 | bytes 16795656 | tf_op jit(solution)/shard_map/add | solution.py:50
  (3 shorter events, 0.0 us)
Async XLA Ops:
  7.2 108.7 %all-gather.2.cloned.1.call-start = ((), (), s32[]{:S(2)}) async-start(), calls=%async_computation.1 | async-start | bytes 2228224 | tf_op jit(solution)/shard_map/all_gather | solution.py:31
  55.4 49.9 %all-to-all-start = ((bf16[16,16,512]{2,0,1:T(8,128)(2,1)}), bf16[16,16,512]{2,0,1:T(8,128)(2,1)S(1)}, u32[]{:S(2)}, u32[]{:S(2)}) async-start(bf16[16,16,512]{2,0,1:T(8,128)(2,1)} %bitcast.8), calls=%async_computation | async-start | bytes 524288 | tf_op jit(solution)/shard_map/all_to_all | solution.py:27
Sparse Core Ops, SparseCore 0:
  54.8 61.1 all-gather.1
where the time goes:
time: 181 us; the launch traced here: 180 us
  blocking collectives  124 us (69%)
  between operations  18.5 us (10%)
  other arithmetic  12 us (7%)
  waiting for transfers between devices  10.7 us (6%)
  matrix products  6.84 us (4%)
  starting transfers between devices  5.46 us (3%)
  local copies, waits for them, and re-layouts  2 us (1%)
    psum x2, blocking collectives, on_device(): lax.psum((trace_part, fourth_part), ('scen', 'fac'))  80.2 us
    psum x1, blocking collectives, on_device(): lax.psum(jnp.sum(scenarios.astype(jnp.float32), axis=0), ('scen', 'fac'))  42.1 us
    all_gather x1, waiting for transfers between devices, on_device(): lax.all_gather(wide_cols, 'scen', axis=0, tiled=True)  10.7 us
    add x1, other arithmetic, on_device(): shrunk = (1.0 - shrinkage) * covariance + shrinkage * mu_scale * diag_mask  8.69 us
    dot_general x1, matrix products, on_device(): lax.dot_general(narrow_all, lax.all_gather(wide_cols, 'scen', axis=0, til...  6.84 us
    all_to_all x1, starting transfers between devices, on_device(): lax.all_to_all(local_rows, 'scen', split_axis=1, concat_axis=0, tiled=True)  5.42 us
  transfers between devices with their start and end apart: 2, of which 1 were waited for; matrix products, arithmetic and copies ran while one was open for 1% of the time, Pallas kernels for 0%

commit v1 on v0

--- a/solution.py
+++ b/solution.py
@@ -14,7 +14,7 @@
     block_width = factors // fac_size
     owner_idx = lax.axis_index("scen")
     block_idx = lax.axis_index("fac")
-    col_total = lax.psum(jnp.sum(scenarios.astype(jnp.float32), axis=0), ("scen", "fac"))
+    col_total = lax.psum(lax.psum(jnp.sum(scenarios.astype(jnp.float32), axis=0), "fac"), "scen")
     col_mean = col_total / total_rows
     centered = (scenarios.astype(jnp.float32) - col_mean).astype(jnp.bfloat16)
     as_float = centered.astype(jnp.float32)

time: 181 us -> 217 us (1.20)
  blocking collectives: 124 us -> 164 us
    psum x1 -> x2, blocking collectives: 42.1 us -> 82 us  [the longest x1 78.2 us: on_device(): lax.psum(lax.psum(jnp.sum(scenarios.astype(jnp.float32), axis=0), 'fac'),...]
where the time goes in v1:
time: 217 us
  blocking collectives  164 us (76%)
  between operations  18.5 us (9%)
  other arithmetic  12 us (6%)
  waiting for transfers between devices  9.5 us (4%)
  matrix products  6.85 us (3%)
  starting transfers between devices  3.57 us (2%)
    psum x2, blocking collectives, on_device(): lax.psum((trace_part, fourth_part), ('scen', 'fac'))  80.4 us
    psum x1, blocking collectives, on_device(): lax.psum(lax.psum(jnp.sum(scenarios.astype(jnp.float32), axis=0), 'fac'),...  78.2 us
    all_gather x1, waiting for transfers between devices, on_device(): lax.all_gather(wide_cols, 'scen', axis=0, tiled=True)  9.48 us
    add x1, other arithmetic, on_device(): shrunk = (1.0 - shrinkage) * covariance + shrinkage * mu_scale * diag_mask  8.69 us
    dot_general x1, matrix products, on_device(): lax.dot_general(narrow_all, lax.all_gather(wide_cols, 'scen', axis=0, til...  6.85 us
  transfers between devices with their start and end apart: 2, of which 1 were waited for; matrix products, arithmetic and copies ran while one was open for 1% of the time, Pallas kernels for 0%

profile of v1, /device:TPU:0, one launch (start us, length us, event | category | flops | bytes accessed | tf_op | source)
XLA Modules:
  0.0 216.8 jit_solution(9123366329811911607)
XLA Ops:
  7.2 0.0 all-gather.2.cloned.1.call-start
  7.2 1.0 convert_reduce_fusion
  8.2 3.7 %psum.35 = f32[8192]{0:T(1024)S(1)} all-reduce(f32[8192]{0:T(1024)S(1)} %convert_reduce_fusion), channel_id=1, replica_groups=mesh['scen'=16,'fac'=2] {'fac'}, use_global_device_ids=true, to_apply=%region_1.0 | all-reduce | flops 8192 | bytes 65536 | tf_op jit(solution)/shard_map/psum | solution.py:17
  11.9 78.2 %psum.36 = f32[8192]{0:T(1024)S(1)} all-reduce(f32[8192]{0:T(1024)S(1)} %psum.35), channel_id=1, replica_groups=mesh['scen'=16,'fac'=2] {'scen'}, use_global_device_ids=true, to_apply=%region_2.0 | all-reduce | flops 8192 | bytes 65536 | tf_op jit(solution)/shard_map/psum | solution.py:17
  90.2 1.6 fusion.5
  91.8 2.0 all_gather.6
  93.8 0.7 constant_dynamic-slice_fusion
  94.5 0.0 all-gather.2.cloned.1.call-update
  94.5 0.7 copy.8
  95.2 3.5 %all-to-all-start = ((bf16[16,16,512]{2,0,1:T(8,128)(2,1)}), bf16[16,16,512]{2,0,1:T(8,128)(2,1)S(1)}, u32[]{:S(2)}, u32[]{:S(2)}) async-start(bf16[16,16,512]{2,0,1:T(8,128)(2,1)} %bitcast.8), calls=%async_computation | async-start | bytes 524288 | tf_op jit(solution)/shard_map/all_to_all | solution.py:27
  98.8 41.1 %psum.38 = f32[]{:T(128)} all-reduce(f32[]{:T(128)} %get-tuple-element.3), channel_id=1, replica_groups=mesh['scen'=16,'fac'=2] {'scen','fac'}, use_global_device_ids=true, to_apply=%region_7.0 | all-reduce | flops 1 | bytes 8 | tf_op jit(solution)/shard_map/psum | solution.py:24
  139.8 0.6 dynamic_slice.7
  142.4 0.7 multiply_reduce_fusion
  143.1 0.0 all-to-all-done
  143.1 9.5 %all-gather.2.cloned.1.call-done = bf16[256,4096]{1,0:T(8,128)(2,1)} async-done(((bf16[16,4096]{1,0:T(8,128)(2,1)}), bf16[256,4096]{1,0:T(8,128)(2,1)}) %all-gather.2.cloned.1.call-update) | async-done | bytes 2097168 | tf_op jit(solution)/shard_map/all_gather | solution.py:31
  152.5 6.9 %fusion.2 = (f32[]{:T(128)}, f32[512,4096]{1,0:T(8,128)}) fusion(f32[]{:T(128)S(6)} %div.32, s32[4096]{0:T(1024)S(1)} %iota_add_fusion, s32[512]{0:T(512)S(1)} %iota_add_fusion.1, bf16[256,512]{1,0:T(8,128)(2,1)S(1)} %bitcast.10, bf16[256,4096]{1,0:T(8,128)(2,1)} %all-gather.2.cloned.1.call-done), kind=kOutput, calls=%fused_computation.4 | convolution fusion | flops 1086324736 | bytes 10766344 | tf_op jit(solution)/shard_map/dot_general | solution.py:29
  159.4 39.3 %all-reduce = (f32[]{:T(128)}, f32[]{:T(128)}) all-reduce(f32[]{:T(128)} %multiply_reduce_fusion, f32[]{:T(128)} %get-tuple-element.8), channel_id=1, replica_groups=mesh['scen'=16,'fac'=2] {'scen','fac'}, use_global_device_ids=true, to_apply=%region_5.0 | all-reduce | flops 2 | bytes 16 | tf_op jit(solution)/shard_map/psum | solution.py:24
  200.1 8.7 %fusion.3 = f32[512,4096]{1,0:T(8,128)} fusion(f32[512,4096]{1,0:T(8,128)} %get-tuple-element.9, f32[]{:T(128)S(6)} %mul.61, f32[]{:T(128)S(6)} %mul.58, s32[4096]{0:T(1024)S(1)} %iota_add_fusion, s32[512]{0:T(512)S(1)} %iota_add_fusion.1), kind=kLoop, calls=%fused_computation.5 | loop fusion | flops 8388608 | bytes 16795656 | tf_op jit(solution)/shard_map/add | solution.py:50
  (3 shorter events, 0.0 us)
Async XLA Ops:
  7.2 145.4 %all-gather.2.cloned.1.call-start = ((), (), s32[]{:S(2)}) async-start(), calls=%async_computation.1 | async-start | bytes 2228224 | tf_op jit(solution)/shard_map/all_gather | solution.py:31
  95.2 47.9 %all-to-all-start = ((bf16[16,16,512]{2,0,1:T(8,128)(2,1)}), bf16[16,16,512]{2,0,1:T(8,128)(2,1)S(1)}, u32[]{:S(2)}, u32[]{:S(2)}) async-start(bf16[16,16,512]{2,0,1:T(8,128)(2,1)} %bitcast.8), calls=%async_computation | async-start | bytes 524288 | tf_op jit(solution)/shard_map/all_to_all | solution.py:27
Sparse Core Ops, SparseCore 0:
  94.6 57.9 all-gather.1

commit v2 on v0

--- a/solution.py
+++ b/solution.py
@@ -14,7 +14,9 @@
     block_width = factors // fac_size
     owner_idx = lax.axis_index("scen")
     block_idx = lax.axis_index("fac")
-    col_total = lax.psum(jnp.sum(scenarios.astype(jnp.float32), axis=0), ("scen", "fac"))
+    col_total = jnp.sum(
+        lax.all_gather(jnp.sum(scenarios.astype(jnp.float32), axis=0), ("scen", "fac")), axis=0
+    )
     col_mean = col_total / total_rows
     centered = (scenarios.astype(jnp.float32) - col_mean).astype(jnp.bfloat16)
     as_float = centered.astype(jnp.float32)

time: 181 us -> 199 us (1.099)
  waiting for transfers between devices: 10.7 us -> 69.8 us
  blocking collectives: 124 us -> 82 us
    all_gather x0 -> x1, waiting for transfers between devices: none -> 58.9 us  [on_device(): lax.all_gather(jnp.sum(scenarios.astype(jnp.float32), axis=0), ('scen', '...]
    psum x1 -> x0, blocking collectives: 42.1 us -> none  [on_device(): lax.psum(jnp.sum(scenarios.astype(jnp.float32), axis=0), ('scen', 'fac'))]
  transfers between devices with their start and end apart: 2 -> 3, of which waited for: 1 -> 2; matrix products, arithmetic and copies ran while one was open for 1% -> 1% of each run, Pallas kernels for 0% -> 0%
where the time goes in v2:
time: 199 us; the launch traced here: 198 us
  blocking collectives  82 us (41%)
  waiting for transfers between devices  69.8 us (35%)
  between operations  18.6 us (9%)
  other arithmetic  12.7 us (6%)
  matrix products  6.85 us (3%)
  starting transfers between devices  4.68 us (2%)
  local copies, waits for them, and re-layouts  3.42 us (2%)
    psum x2, blocking collectives, on_device(): lax.psum((trace_part, fourth_part), ('scen', 'fac'))  80.1 us
    all_gather x1, waiting for transfers between devices, on_device(): lax.all_gather(jnp.sum(scenarios.astype(jnp.float32), axis=0), ('scen', '...  58.9 us
    all_gather x1, waiting for transfers between devices, on_device(): lax.all_gather(wide_cols, 'scen', axis=0, tiled=True)  10.9 us
    add x1, other arithmetic, on_device(): shrunk = (1.0 - shrinkage) * covariance + shrinkage * mu_scale * diag_mask  8.69 us
    dot_general x1, matrix products, on_device(): lax.dot_general(narrow_all, lax.all_gather(wide_cols, 'scen', axis=0, til...  6.85 us
    all_to_all x1, starting transfers between devices, on_device(): lax.all_to_all(local_rows, 'scen', split_axis=1, concat_axis=0, tiled=True)  4.6 us
  transfers between devices with their start and end apart: 3, of which 2 were waited for; matrix products, arithmetic and copies ran while one was open for 1% of the time, Pallas kernels for 0%

profile of v2, /device:TPU:0, one launch (start us, length us, event | category | flops | bytes accessed | tf_op | source)
XLA Modules:
  0.0 198.1 jit_solution(18300053924276771151)
XLA Ops:
  7.2 0.0 all-gather.6.cloned.1.call-start
  7.2 1.6 convert_reduce_fusion
  8.8 0.0 all-gather.6.cloned.1.call-update
  8.8 0.0 all-gather.4.cloned.1.call-start
  8.9 58.9 %all-gather.6.cloned.1.call-done = f32[262144]{0:T(1024)} async-done(((f32[8192]{0:T(1024)}), f32[262144]{0:T(1024)}) %all-gather.6.cloned.1.call-update) | async-done | bytes 1048592 | tf_op jit(solution)/shard_map/all_gather | solution.py:18
  67.8 1.4 reshape.12
  69.2 0.1 reduce_sum.55
  69.3 1.6 fusion.5
  70.9 2.0 %all_gather.14 = bf16[16,8192]{1,0:T(8,128)(2,1)S(1)} all-gather(bf16[8,8192]{1,0:T(8,128)(2,1)S(1)} %get-tuple-element.7), channel_id=1, replica_groups=mesh['scen'=16,'fac'=2] {'fac'}, dimensions={0}, use_global_device_ids=true | all-gather | bytes 393216 | tf_op jit(solution)/shard_map/all_gather | solution.py:28
  72.9 0.7 constant_dynamic-slice_fusion
  73.6 0.0 all-gather.4.cloned.1.call-update
  73.6 0.7 copy.9
  74.3 4.6 %all-to-all-start = ((bf16[16,16,512]{2,0,1:T(8,128)(2,1)}), bf16[16,16,512]{2,0,1:T(8,128)(2,1)S(1)}, u32[]{:S(2)}, u32[]{:S(2)}) async-start(bf16[16,16,512]{2,0,1:T(8,128)(2,1)} %bitcast.8), calls=%async_computation | async-start | bytes 524288 | tf_op jit(solution)/shard_map/all_to_all | solution.py:29
  79.0 41.1 %psum.22 = f32[]{:T(128)} all-reduce(f32[]{:T(128)} %get-tuple-element.3), channel_id=1, replica_groups=mesh['scen'=16,'fac'=2] {'scen','fac'}, use_global_device_ids=true, to_apply=%region_6.0 | all-reduce | flops 1 | bytes 8 | tf_op jit(solution)/shard_map/psum | solution.py:26
  120.1 0.6 dynamic_slice.7
  122.6 0.7 multiply_reduce_fusion
  123.3 0.0 all-to-all-done
  123.3 10.9 %all-gather.4.cloned.1.call-done = bf16[256,4096]{1,0:T(8,128)(2,1)} async-done(((bf16[16,4096]{1,0:T(8,128)(2,1)}), bf16[256,4096]{1,0:T(8,128)(2,1)}) %all-gather.4.cloned.1.call-update) | async-done | bytes 2097168 | tf_op jit(solution)/shard_map/all_gather | solution.py:33
  134.2 6.9 %fusion.2 = (f32[]{:T(128)}, f32[512,4096]{1,0:T(8,128)}) fusion(f32[]{:T(128)S(6)} %div.32, s32[4096]{0:T(1024)S(1)} %iota_add_fusion, s32[512]{0:T(512)S(1)} %iota_add_fusion.1, bf16[256,512]{1,0:T(8,128)(2,1)S(1)} %bitcast.10, bf16[256,4096]{1,0:T(8,128)(2,1)} %all-gather.4.cloned.1.call-done), kind=kOutput, calls=%fused_computation.4 | convolution fusion | flops 1086324736 | bytes 10766344 | tf_op jit(solution)/shard_map/dot_general | solution.py:31
  141.1 38.9 %all-reduce = (f32[]{:T(128)}, f32[]{:T(128)}) all-reduce(f32[]{:T(128)} %multiply_reduce_fusion, f32[]{:T(128)} %get-tuple-element.8), channel_id=1, replica_groups=mesh['scen'=16,'fac'=2] {'scen','fac'}, use_global_device_ids=true, to_apply=%region_4.0 | all-reduce | flops 2 | bytes 16 | tf_op jit(solution)/shard_map/psum | solution.py:26
  181.4 8.7 %fusion.3 = f32[512,4096]{1,0:T(8,128)} fusion(f32[512,4096]{1,0:T(8,128)} %get-tuple-element.9, f32[]{:T(128)S(6)} %mul.61, f32[]{:T(128)S(6)} %mul.58, s32[4096]{0:T(1024)S(1)} %iota_add_fusion, s32[512]{0:T(512)S(1)} %iota_add_fusion.1), kind=kLoop, calls=%fused_computation.5 | loop fusion | flops 8388608 | bytes 16795656 | tf_op jit(solution)/shard_map/add | solution.py:52
  (3 shorter events, 0.0 us)
Async XLA Ops:
  7.2 60.6 %all-gather.6.cloned.1.call-start = ((), (), s32[]{:S(2)}) async-start(), calls=%async_computation.2 | async-start | bytes 1081344 | tf_op jit(solution)/shard_map/all_gather | solution.py:18
  8.8 125.4 %all-gather.4.cloned.1.call-start = ((), (), s32[]{:S(2)}) async-start(), calls=%async_computation.1 | async-start | bytes 2228224 | tf_op jit(solution)/shard_map/all_gather | solution.py:33
  74.3 49.0 %all-to-all-start = ((bf16[16,16,512]{2,0,1:T(8,128)(2,1)}), bf16[16,16,512]{2,0,1:T(8,128)(2,1)S(1)}, u32[]{:S(2)}, u32[]{:S(2)}) async-start(bf16[16,16,512]{2,0,1:T(8,128)(2,1)} %bitcast.8), calls=%async_computation | async-start | bytes 524288 | tf_op jit(solution)/shard_map/all_to_all | solution.py:29
Sparse Core Ops, SparseCore 0:
  11.4 56.3 all-gather.5
  73.7 60.4 all-gather.3

commit v3 on v0

--- a/solution.py
+++ b/solution.py
@@ -21,7 +21,7 @@
     squared = jnp.sum(as_float * as_float, axis=1)
     trace_part = jnp.sum(squared)
     fourth_part = jnp.sum(squared * squared)
-    trace_total, fourth_total = lax.psum((trace_part, fourth_part), ("scen", "fac"))
+    trace_total, fourth_total = lax.psum(lax.psum((trace_part, fourth_part), "fac"), "scen")
     contract = (((0,), (0,)), ((), ()))
     local_rows = lax.all_gather(centered, "fac", axis=0, tiled=True)
     narrow_all = lax.all_to_all(local_rows, "scen", split_axis=1, concat_axis=0, tiled=True)

time: 181 us -> 180 us (level)
  waiting for transfers between devices: 10.7 us -> 4.54 us
  blocking collectives: 124 us -> 130 us
    all_gather x1, waiting for transfers between devices: 10.7 us -> 4.52 us  [on_device(): lax.all_gather(wide_cols, 'scen', axis=0, tiled=True)]
    psum x2 -> x3, blocking collectives: 80.2 us -> 85.7 us  [the longest x1 43.3 us: on_device(): lax.psum(lax.psum((trace_part, fourth_part), 'fac'), 'scen')]
where the time goes in v3:
time: 180 us; the launch traced here: 179 us
  blocking collectives  130 us (72%)
  between operations  18.5 us (10%)
  other arithmetic  11.9 us (7%)
  matrix products  6.85 us (4%)
  starting transfers between devices  5.46 us (3%)
  waiting for transfers between devices  4.54 us (3%)
  local copies, waits for them, and re-layouts  2 us (1%)
    psum x1, blocking collectives, on_device(): lax.psum(lax.psum((trace_part, fourth_part), 'fac'), 'scen')  43.3 us
    psum x1, blocking collectives, on_device(): lax.psum(jnp.sum(scenarios.astype(jnp.float32), axis=0), ('scen', 'fac'))  42.1 us
    psum x1, blocking collectives, on_device(): frob_sum = lax.psum(jnp.sum(distance * distance), ('scen', 'fac'))  39.4 us
    add x1, other arithmetic, on_device(): shrunk = (1.0 - shrinkage) * covariance + shrinkage * mu_scale * diag_mask  8.69 us
    dot_general x1, matrix products, on_device(): lax.dot_general(narrow_all, lax.all_gather(wide_cols, 'scen', axis=0, til...  6.85 us
    all_to_all x1, starting transfers between devices, on_device(): lax.all_to_all(local_rows, 'scen', split_axis=1, concat_axis=0, tiled=True)  5.42 us
    all_gather x1, waiting for transfers between devices, on_device(): lax.all_gather(wide_cols, 'scen', axis=0, tiled=True)  4.52 us
  transfers between devices with their start and end apart: 2, of which 1 were waited for; matrix products, arithmetic and copies ran while one was open for 1% of the time, Pallas kernels for 0%

profile of v3, /device:TPU:0, one launch (start us, length us, event | category | flops | bytes accessed | tf_op | source)
XLA Modules:
  0.0 179.2 jit_solution(16003750519661413964)
XLA Ops:
  7.2 0.0 all-gather.2.cloned.1.call-start
  7.2 1.0 convert_reduce_fusion
  8.2 42.1 %psum.42 = f32[8192]{0:T(1024)S(1)} all-reduce(f32[8192]{0:T(1024)S(1)} %convert_reduce_fusion), channel_id=1, replica_groups=mesh['scen'=16,'fac'=2] {'scen','fac'}, use_global_device_ids=true, to_apply=%region_1.0 | all-reduce | flops 8192 | bytes 65536 | tf_op jit(solution)/shard_map/psum | solution.py:17
  50.4 1.6 fusion.5
  52.0 2.0 %all_gather.6 = bf16[16,8192]{1,0:T(8,128)(2,1)S(1)} all-gather(bf16[8,8192]{1,0:T(8,128)(2,1)S(1)} %get-tuple-element.9), channel_id=1, replica_groups=mesh['scen'=16,'fac'=2] {'fac'}, dimensions={0}, use_global_device_ids=true | all-gather | bytes 393216 | tf_op jit(solution)/shard_map/all_gather | solution.py:26
  54.0 0.7 constant_dynamic-slice_fusion
  54.6 0.0 all-gather.2.cloned.1.call-update
  54.6 0.7 copy.8
  55.4 5.4 %all-to-all-start = ((bf16[16,16,512]{2,0,1:T(8,128)(2,1)}), bf16[16,16,512]{2,0,1:T(8,128)(2,1)S(1)}, u32[]{:S(2)}, u32[]{:S(2)}) async-start(bf16[16,16,512]{2,0,1:T(8,128)(2,1)} %bitcast.8), calls=%async_computation | async-start | bytes 524288 | tf_op jit(solution)/shard_map/all_to_all | solution.py:27
  60.8 0.6 multiply_reduce_fusion
  61.4 3.1 %all-reduce.1 = (f32[]{:T(128)}, f32[]{:T(128)}) all-reduce(f32[]{:T(128)} %multiply_reduce_fusion, f32[]{:T(128)} %get-tuple-element.3), channel_id=1, replica_groups=mesh['scen'=16,'fac'=2] {'fac'}, use_global_device_ids=true, to_apply=%region_4.0 | all-reduce | flops 2 | bytes 16 | tf_op jit(solution)/shard_map/psum | solution.py:24
  64.5 43.3 %all-reduce = (f32[]{:T(128)}, f32[]{:T(128)}) all-reduce(f32[]{:T(128)} %get-tuple-element.7, f32[]{:T(128)} %get-tuple-element.8), channel_id=1, replica_groups=mesh['scen'=16,'fac'=2] {'scen'}, use_global_device_ids=true, to_apply=%region_5.0 | all-reduce | flops 2 | bytes 16 | tf_op jit(solution)/shard_map/psum | solution.py:24
  107.8 0.6 dynamic_slice.7
  111.0 0.0 all-to-all-done
  111.0 4.5 %all-gather.2.cloned.1.call-done = bf16[256,4096]{1,0:T(8,128)(2,1)} async-done(((bf16[16,4096]{1,0:T(8,128)(2,1)}), bf16[256,4096]{1,0:T(8,128)(2,1)}) %all-gather.2.cloned.1.call-update) | async-done | bytes 2097168 | tf_op jit(solution)/shard_map/all_gather | solution.py:31
  115.6 6.8 %fusion.2 = (f32[]{:T(128)}, f32[512,4096]{1,0:T(8,128)}) fusion(f32[]{:T(128)S(6)} %div.32, s32[4096]{0:T(1024)S(1)} %iota_add_fusion, s32[512]{0:T(512)S(1)} %iota_add_fusion.1, bf16[256,512]{1,0:T(8,128)(2,1)S(1)} %bitcast.10, bf16[256,4096]{1,0:T(8,128)(2,1)} %all-gather.2.cloned.1.call-done), kind=kOutput, calls=%fused_computation.4 | convolution fusion | flops 1086324736 | bytes 10766344 | tf_op jit(solution)/shard_map/dot_general | solution.py:29
  122.4 39.4 %psum.47 = f32[]{:T(128)} all-reduce(f32[]{:T(128)} %get-tuple-element.10), channel_id=1, replica_groups=mesh['scen'=16,'fac'=2] {'scen','fac'}, use_global_device_ids=true, to_apply=%region_10.0 | all-reduce | flops 1 | bytes 8 | tf_op jit(solution)/shard_map/psum | solution.py:45
  162.5 8.7 %fusion.3 = f32[512,4096]{1,0:T(8,128)} fusion(f32[512,4096]{1,0:T(8,128)} %get-tuple-element.11, f32[]{:T(128)S(6)} %mul.61, f32[]{:T(128)S(6)} %mul.58, s32[4096]{0:T(1024)S(1)} %iota_add_fusion, s32[512]{0:T(512)S(1)} %iota_add_fusion.1), kind=kLoop, calls=%fused_computation.5 | loop fusion | flops 8388608 | bytes 16795656 | tf_op jit(solution)/shard_map/add | solution.py:50
  (3 shorter events, 0.0 us)
Async XLA Ops:
  7.2 108.4 %all-gather.2.cloned.1.call-start = ((), (), s32[]{:S(2)}) async-start(), calls=%async_computation.1 | async-start | bytes 2228224 | tf_op jit(solution)/shard_map/all_gather | solution.py:31
  55.4 55.6 %all-to-all-start = ((bf16[16,16,512]{2,0,1:T(8,128)(2,1)}), bf16[16,16,512]{2,0,1:T(8,128)(2,1)S(1)}, u32[]{:S(2)}, u32[]{:S(2)}) async-start(bf16[16,16,512]{2,0,1:T(8,128)(2,1)} %bitcast.8), calls=%async_computation | async-start | bytes 524288 | tf_op jit(solution)/shard_map/all_to_all | solution.py:27
Sparse Core Ops, SparseCore 0:
  54.8 60.7 all-gather.1
